TPU v7x, 256 devices: a whole 4x4x8 slice. The times are simulated.
256 devices in a mesh: section: 4 (over y), gy: 8 (over z), gx: 8 (over x, core).
Axes of the slice: x: 4, y: 4, z: 8, core: 2. Of those that a mesh axis runs over, the one named last changes fastest.
Arguments:
- level_input: bfloat16 [4, 4, 64, 128, 320], P('section', None, 'gy', 'gx'), may hold values from -72 to 72, as said below
- out_grad: bfloat16 [4, 4, 64, 128, 320], P('section', None, 'gy', 'gx'), may hold values from -6 to 6
- conv_weight: bfloat16 [4, 27, 320, 320], P('section'), may hold values from -0.0625 to 0.0625
- norm_gain: float32 [4, 320], P('section'), may hold values from 0.1 to 1.9
- norm_shift: float32 [4, 320], P('section'), may hold values from -3 to 3
Outputs:
- upstream_grad: bfloat16 [4, 4, 64, 128, 320], P('section', None, 'gy', 'gx')
- weight_grad: float32 [4, 8640, 320], P('section', ('gy', 'gx'))
- param_grad: float32 [4, 3, 320], P('section')
Inputs may be any that keep to these rules, and one draw needn't show every extreme that they name: `level_input`: level input values of order one with varying channel and position scales.
All inputs are finite; a program needn't handle non-finite values.
Results may differ from a plain program's by a relative error of at most 0.0029.
Values may be sent and summed in bfloat16 or wider, within the bound.
A program may use at most 128 MiB of HBM per device.

v0:
```python
import jax
import jax.numpy as jnp
from jax import lax
from jax.sharding import PartitionSpec as P

G = 32
eps = 1e-05


def from_everyone(shard, axis):
    count = lax.axis_size(axis)
    return lax.all_to_all(
        jnp.broadcast_to(shard[None], (count, *shard.shape)), axis, 0, 0, tiled=True
    )


def taken_together(shard, axis):
    everything = from_everyone(shard, axis)
    return jnp.sum(everything, axis=0)


def packed_total(arrays, axis):
    line, at, done = (jnp.concatenate([a.reshape(-1) for a in arrays]), 0, [])
    subtotal = taken_together(line, axis)
    for a in arrays:
        done.append(subtotal[at : at + a.size].reshape(a.shape))
        at += a.size
    return tuple(done)


def padded(block, sides, width):
    for axis, dim in sides:
        count = lax.axis_size(axis)
        forward = [(i, i + 1) for i in range(count - 1)]
        backward = [(target, source) for source, target in forward]
        low = lax.ppermute(
            lax.slice_in_dim(block, block.shape[dim] - width, None, axis=dim), axis, forward
        )
        high = lax.ppermute(lax.slice_in_dim(block, 0, width, axis=dim), axis, backward)
        block = jnp.concatenate([low, block, high], axis=dim)
    return block


def in_one(arrays, axis):
    ends = [0]
    for a in arrays:
        ends.append(ends[-1] + a.size)
    subtotal = lax.psum(jnp.concatenate([a.ravel() for a in arrays]), axis)
    return tuple((subtotal[b:e].reshape(a.shape) for a, b, e in zip(arrays, ends, ends[1:])))


def passed_along(shard, axis, by):
    count = lax.axis_size(axis)
    pairs = [(i, i + by) for i in range(count) if 0 <= i + by < count]
    return lax.ppermute(shard, axis, pairs)


def expand_groups(values, groups, per_group):
    return jnp.broadcast_to(values[:, None], (groups, per_group)).reshape(groups * per_group)


def local(level_input, out_grad, conv_weight, norm_gain, norm_shift):
    level_x = level_input[0]
    grad_cells = out_grad[0]
    kernel_all = conv_weight[0]
    gain_vec = norm_gain[0]
    shift_vec = norm_shift[0]
    frames, rows_h, cols_w, channels = level_x.shape
    groups = G
    per_group = channels // groups
    cell_count = frames * rows_h * cols_w
    members = cell_count * per_group * lax.axis_size("gy") * lax.axis_size("gx")
    x_float = level_x.astype(jnp.float32).reshape(cell_count, groups, per_group)
    sum_first, sum_second = packed_total(
        (jnp.sum(x_float, axis=(0, 2)), jnp.sum(x_float * x_float, axis=(0, 2))), ("gy", "gx")
    )
    group_mean = sum_first / members
    group_var = sum_second / members - group_mean * group_mean
    centered = x_float - group_mean[None, :, None]
    inv_std = 1.0 / jnp.sqrt(group_var + eps)
    normed = (centered * inv_std[None, :, None]).reshape(cell_count, channels)
    activ = normed * gain_vec[None, :] + shift_vec[None, :]
    sigmoid_v = jax.nn.sigmoid(activ)
    unit_rows = (activ * sigmoid_v).astype(jnp.bfloat16)
    extended = padded(grad_cells, (("gy", 1), ("gx", 2)), 1)
    framed = jnp.pad(extended, ((1, 1), (0, 0), (0, 0), (0, 0)))
    weight_pieces = []
    input_side = jnp.zeros((cell_count, channels), jnp.float32)
    for offset_f in range(3):
        for offset_h in range(3):
            for offset_w in range(3):
                kernel_idx = offset_f * 9 + offset_h * 3 + offset_w
                window = framed[
                    2 - offset_f : 2 - offset_f + frames,
                    2 - offset_h : 2 - offset_h + rows_h,
                    2 - offset_w : 2 - offset_w + cols_w,
                    :,
                ].reshape(cell_count, channels)
                input_side = input_side + lax.dot_general(
                    window,
                    kernel_all[kernel_idx],
                    (((1,), (1,)), ((), ())),
                    preferred_element_type=jnp.float32,
                )
                weight_pieces.append(
                    lax.dot_general(
                        unit_rows,
                        window,
                        (((0,), (0,)), ((), ())),
                        preferred_element_type=jnp.float32,
                    )
                )
    weight_part = lax.psum_scatter(
        jnp.concatenate(weight_pieces, axis=0), ("gy", "gx"), scatter_dimension=0, tiled=True
    )
    silu_slope = sigmoid_v * (1.0 + activ * (1.0 - sigmoid_v))
    act_grad = input_side * silu_slope
    grad_float = grad_cells.astype(jnp.float32).reshape(cell_count, channels)
    gain_sum, shift_sum, bias_sum = in_one(
        (
            jnp.sum(act_grad * normed, axis=0),
            jnp.sum(act_grad, axis=0),
            jnp.sum(grad_float, axis=0),
        ),
        ("gy", "gx"),
    )
    mean_first = jnp.sum((gain_vec * shift_sum).reshape(groups, per_group), axis=1) / members
    mean_second = jnp.sum((gain_vec * gain_sum).reshape(groups, per_group), axis=1) / members
    norm_grad = (
        act_grad * gain_vec[None, :]
        - expand_groups(mean_first, groups, per_group)[None, :]
        - normed * expand_groups(mean_second, groups, per_group)[None, :]
    ) * expand_groups(inv_std, groups, per_group)[None, :]
    level_grad = (
        (grad_float + norm_grad).astype(jnp.bfloat16).reshape(1, frames, rows_h, cols_w, channels)
    )
    upstream_grad = passed_along(level_grad, "section", -1)
    param_grad = jnp.stack([gain_sum, shift_sum, bias_sum])[None]
    return (upstream_grad, weight_part[None], param_grad)


def solution(mesh):
    return jax.shard_map(
        local,
        mesh=mesh,
        in_specs=(
            P("section", None, "gy", "gx", None),
            P("section", None, "gy", "gx", None),
            P("section", None, None, None),
            P("section", None),
            P("section", None),
        ),
        out_specs=(
            P("section", None, "gy", "gx", None),
            P("section", ("gy", "gx"), None),
            P("section", None, None),
        ),
        check_vma=False,
    )
```

profile of v0, /device:TPU:2, one launch (start us, length us, event | category | flops | bytes accessed | tf_op | source)
XLA Modules:
  0.0 333.8 jit_solution(14471769354519032061)
XLA Ops:
  9.5 12.0 %all-to-all-start = ((f32[64,1,64]{2,1,0:T(1,128)}), f32[64,1,64]{2,1,0:T(1,128)S(1)}, u32[]{:S(2)}, u32[]{:S(2)}) async-start(f32[64,1,64]{2,1,0:T(1,128)} %broadcast_in_dim.10), calls=%async_computation | async-start | bytes 65536 | tf_op jit(solution)/shard_map/all_to_all | solution.py:12
  23.8 4.5 %collective-permute-start = (bf16[4,1,16,320]{3,2,1,0:T(8,128)(2,1)S(1)}, bf16[4,1,16,320]{3,2,1,0:T(8,128)(2,1)S(1)}, u32[]{:S(2)}, u32[]{:S(2)}) collective-permute-start(bf16[4,1,16,320]{3,2,1,0:T(8,128)(2,1)S(1)} %get-tuple-element.54), channel_id=1, source_target_pairs={{0,8},{8,16},{16,24},{24,32},{32,40},{40,48},{48,56},{1,9},{9,17},... | collective-permute-start | bytes 122888 | tf_op jit(solution)/shard_map/ppermute | solution.py:36
  28.3 1.7 convert_reduce_fusion
  30.0 2.0 copy.26
  33.4 1.9 copy.24
  37.2 2.2 convolution_bitcast_fusion
  40.6 1.9 collective-permute-start.3
  42.5 2.4 collective-permute-start.2
  49.1 1.9 fusion.68
  54.2 2.5 fusion.26
  76.4 1.3 convolution_add_fusion.16
  78.9 2.2 convolution_add_fusion.15
  96.5 14.0 %concatenate.39 = f32[8640,320]{0,1:T(8,128)} concatenate(f32[320,320]{0,1:T(8,128)} %fusion.73, f32[320,320]{0,1:T(8,128)} %fusion.74, f32[320,320]{0,1:T(8,128)} %fusion.75, f32[320,320]{0,1:T(8,128)} %fusion.76, f32[320,320]{0,1:T(8,128)} %fusion.77, f32[320,320]{0,1:T(8,128)} %fusion.78, f32[320,320]{0,1:T(8,128)} %fusion.79, f32[320,320]{0,1:T(8,128)} %fusion.80, ...), dimensions={0} | concatenate | bytes 22118400 | tf_op jit(solution)/shard_map/concatenate | solution.py:114
  110.6 2.0 fusion.3
  112.6 1.4 fusion.19
  114.0 1.4 convolution_add_fusion.13
  115.4 1.3 convolution_add_fusion.12
  116.8 1.3 convolution_add_fusion.11
  118.1 1.3 convolution_add_fusion.10
  119.4 1.3 fusion.2
  120.7 1.3 convolution_add_fusion.8
  122.1 1.4 convolution_add_fusion.7
  123.5 1.3 convolution_add_fusion.6
  124.9 1.3 convolution_add_fusion.5
  126.2 1.4 convolution_add_fusion.4
  127.6 1.3 convolution_add_fusion.3
  129.0 1.3 convolution_add_fusion.2
  130.3 1.3 convolution_add_fusion.1
  131.7 1.6 multiply_reduce_fusion.1
  133.3 122.7 %psum.7 = f32[960]{0:T(1024)S(1)} all-reduce(f32[960]{0:T(1024)S(1)} %pad_maximum_fusion.7), channel_id=1, replica_groups=mesh['section'=4,'gy'=8,'gx'=8] {'gy','gx'}, use_global_device_ids=true, to_apply=%region_8.9 | all-reduce | flops 960 | bytes 7680 | tf_op jit(solution)/shard_map/psum | solution.py:48
  260.6 6.5 %collective-permute-done.4 = bf16[1,4,8,16,320]{4,3,2,1,0:T(8,128)(2,1)S(1)} collective-permute-done((bf16[1,4,8,16,320]{4,3,2,1,0:T(8,128)(2,1)S(1)}, bf16[1,4,8,16,320]{4,3,2,1,0:T(8,128)(2,1)S(1)}, u32[]{:S(2)}, u32[]{:S(2)}) %collective-permute-start.4) | collective-permute-done | bytes 327712 | tf_op jit(solution)/shard_map/ppermute | solution.py:55
  267.1 57.1 %all-reduce.4.cloned.1.call-done = f32[8640,320]{0,1:T(8,128)} async-done(((f32[8640,320]{0,1:T(8,128)}), f32[8640,320]{0,1:T(8,128)}) %all-reduce.4.cloned.1.call-update) | async-done | bytes 11059216
  (146 shorter events, 59.2 us)
Async XLA Ops:
  7.2 41.5 %copy-start = (bf16[1,4,8,16,320]{4,3,2,1,0:T(8,128)(2,1)S(1)}, bf16[1,4,8,16,320]{4,3,2,1,0:T(8,128)(2,1)}, u32[]{:S(2)}) copy-start(bf16[1,4,8,16,320]{4,3,2,1,0:T(8,128)(2,1)} %param.6) | copy-start | bytes 983044
  9.5 25.8 %all-to-all-start = ((f32[64,1,64]{2,1,0:T(1,128)}), f32[64,1,64]{2,1,0:T(1,128)S(1)}, u32[]{:S(2)}, u32[]{:S(2)}) async-start(f32[64,1,64]{2,1,0:T(1,128)} %broadcast_in_dim.10), calls=%async_computation | async-start | bytes 65536 | tf_op jit(solution)/shard_map/all_to_all | solution.py:12
  21.6 302.6 %all-reduce.4.cloned.1.call-start = ((), (), s32[]{:S(2)}) async-start(), calls=%async_computation.1 | async-start | bytes 22282240
  22.5 16.9 %collective-permute-start.1 = (bf16[4,1,16,320]{3,2,1,0:T(8,128)(2,1)S(1)}, bf16[4,1,16,320]{3,2,1,0:T(8,128)(2,1)S(1)}, u32[]{:S(2)}, u32[]{:S(2)}) collective-permute-start(bf16[4,1,16,320]{3,2,1,0:T(8,128)(2,1)S(1)} %get-tuple-element.55), channel_id=1, source_target_pairs={{8,0},{16,8},{24,16},{32,24},{40,32},{48,40},{56,48},{9,1},{17,9},... | collective-permute-start | bytes 122888 | tf_op jit(solution)/shard_map/ppermute | solution.py:39
  23.8 15.6 %collective-permute-start = (bf16[4,1,16,320]{3,2,1,0:T(8,128)(2,1)S(1)}, bf16[4,1,16,320]{3,2,1,0:T(8,128)(2,1)S(1)}, u32[]{:S(2)}, u32[]{:S(2)}) collective-permute-start(bf16[4,1,16,320]{3,2,1,0:T(8,128)(2,1)S(1)} %get-tuple-element.54), channel_id=1, source_target_pairs={{0,8},{8,16},{16,24},{24,32},{32,40},{40,48},{48,56},{1,9},{9,17},... | collective-permute-start | bytes 122888 | tf_op jit(solution)/shard_map/ppermute | solution.py:36
  32.7 9.8 %copy-start.26 = (f32[320]{0:T(512)}, f32[320]{0:T(512)S(1)}, u32[]{:S(2)}) copy-start(f32[320]{0:T(512)S(1)} %reduce.7) | copy-start | bytes 3844
  33.4 9.1 %copy-start.19 = (f32[320]{0:T(512)}, f32[320]{0:T(512)S(1)}, u32[]{:S(2)}) copy-start(f32[320]{0:T(512)S(1)} %reduce.6) | copy-start | bytes 3844
  35.7 6.8 %copy-start.21 = (f32[320]{0:T(512)}, f32[320]{0:T(512)S(1)}, u32[]{:S(2)}) copy-start(f32[320]{0:T(512)S(1)} %mul.173) | copy-start | bytes 3844
  35.9 6.7 %copy-start.23 = (f32[320]{0:T(512)}, f32[320]{0:T(512)S(1)}, u32[]{:S(2)}) copy-start(f32[320]{0:T(512)S(1)} %sub.64) | copy-start | bytes 3844
  39.4 9.2 %copy-start.15 = (bf16[4,1,16,320]{3,2,1,0:T(8,128)(2,1)}, bf16[4,1,16,320]{3,2,1,0:T(8,128)(2,1)S(1)}, u32[]{:S(2)}) copy-start(bf16[4,1,16,320]{3,2,1,0:T(8,128)(2,1)S(1)} %collective-permute-done.1) | copy-start | bytes 122884
  39.4 9.2 %copy-start.17 = (bf16[4,1,16,320]{3,2,1,0:T(8,128)(2,1)}, bf16[4,1,16,320]{3,2,1,0:T(8,128)(2,1)S(1)}, u32[]{:S(2)}) copy-start(bf16[4,1,16,320]{3,2,1,0:T(8,128)(2,1)S(1)} %collective-permute-done) | copy-start | bytes 122884
  40.6 8.0 %collective-permute-start.3 = (bf16[4,10,1,320]{3,2,1,0:T(2,128)(2,1)S(1)}, bf16[4,10,1,320]{3,2,1,0:T(2,128)(2,1)S(1)}, u32[]{:S(2)}, u32[]{:S(2)}) collective-permute-start(bf16[4,10,1,320]{3,2,1,0:T(2,128)(2,1)S(1)} %get-tuple-element.50), channel_id=1, source_target_pairs={{1,0},{2,1},{3,2},{4,3},{5,4},{6,5},{7,6},{9,8},{10,9},{11,10},{12... | collective-permute-start | bytes 76808 | tf_op jit(solution)/shard_map/ppermute | solution.py:39
  42.5 6.0 %collective-permute-start.2 = (bf16[4,10,1,320]{3,2,1,0:T(2,128)(2,1)S(1)}, bf16[4,10,1,320]{3,2,1,0:T(2,128)(2,1)S(1)}, u32[]{:S(2)}, u32[]{:S(2)}) collective-permute-start(bf16[4,10,1,320]{3,2,1,0:T(2,128)(2,1)S(1)} %get-tuple-element.51), channel_id=1, source_target_pairs={{0,1},{1,2},{2,3},{3,4},{4,5},{5,6},{6,7},{8,9},{9,10},{10,11},{11... | collective-permute-start | bytes 76808 | tf_op jit(solution)/shard_map/ppermute | solution.py:36
  51.0 44.3 %copy-start.12 = (bf16[4,8,16,320]{3,2,1,0:T(8,128)(2,1)}, bf16[4,8,16,320]{3,2,1,0:T(8,128)(2,1)S(1)}, u32[]{:S(2)}) copy-start(bf16[4,8,16,320]{3,2,1,0:T(8,128)(2,1)S(1)} %get-tuple-element.24) | copy-start | bytes 983044
  54.2 26.9 %copy-start.9 = (bf16[4,8,16,320]{3,2,1,0:T(8,128)(2,1)}, bf16[4,8,16,320]{3,2,1,0:T(8,128)(2,1)S(1)}, u32[]{:S(2)}) copy-start(bf16[4,8,16,320]{3,2,1,0:T(8,128)(2,1)S(1)} %get-tuple-element.43) | copy-start | bytes 983044
  54.2 28.1 %copy-start.7 = (bf16[4,8,16,320]{3,2,1,0:T(8,128)(2,1)}, bf16[4,8,16,320]{3,2,1,0:T(8,128)(2,1)S(1)}, u32[]{:S(2)}) copy-start(bf16[4,8,16,320]{3,2,1,0:T(8,128)(2,1)S(1)} %get-tuple-element.64) | copy-start | bytes 983044
  54.2 29.3 %copy-start.5 = (bf16[4,8,16,320]{3,2,1,0:T(8,128)(2,1)}, bf16[4,8,16,320]{3,2,1,0:T(8,128)(2,1)S(1)}, u32[]{:S(2)}) copy-start(bf16[4,8,16,320]{3,2,1,0:T(8,128)(2,1)S(1)} %get-tuple-element.42) | copy-start | bytes 983044
  54.2 30.4 %copy-start.4 = (bf16[4,8,16,320]{3,2,1,0:T(8,128)(2,1)}, bf16[4,8,16,320]{3,2,1,0:T(8,128)(2,1)S(1)}, u32[]{:S(2)}) copy-start(bf16[4,8,16,320]{3,2,1,0:T(8,128)(2,1)S(1)} %get-tuple-element.63) | copy-start | bytes 983044
  110.6 6.2 %copy-start.8 = (bf16[4,8,16,320]{3,2,1,0:T(8,128)(2,1)S(1)}, bf16[4,8,16,320]{3,2,1,0:T(8,128)(2,1)}, u32[]{:S(2)}) copy-start(bf16[4,8,16,320]{3,2,1,0:T(8,128)(2,1)} %copy-done.7) | copy-start | bytes 983044
  110.6 7.5 %copy-start.6 = (bf16[4,8,16,320]{3,2,1,0:T(8,128)(2,1)S(1)}, bf16[4,8,16,320]{3,2,1,0:T(8,128)(2,1)}, u32[]{:S(2)}) copy-start(bf16[4,8,16,320]{3,2,1,0:T(8,128)(2,1)} %copy-done.5) | copy-start | bytes 983044
  110.6 8.8 %copy-start.2 = (bf16[4,8,16,320]{3,2,1,0:T(8,128)(2,1)S(1)}, bf16[4,8,16,320]{3,2,1,0:T(8,128)(2,1)}, u32[]{:S(2)}) copy-start(bf16[4,8,16,320]{3,2,1,0:T(8,128)(2,1)} %copy-done.1) | copy-start | bytes 983044
  122.1 9.6 %copy-start.10 = (f32[512,320]{0,1:T(8,128)S(1)}, f32[512,320]{0,1:T(8,128)}, u32[]{:S(2)}) copy-start(f32[512,320]{0,1:T(8,128)} %copy.26) | copy-start | bytes 1966084
  122.1 9.6 %copy-start.13 = (bf16[4,8,16,320]{3,2,1,0:T(8,128)(2,1)S(1)}, bf16[4,8,16,320]{3,2,1,0:T(8,128)(2,1)}, u32[]{:S(2)}) copy-start(bf16[4,8,16,320]{3,2,1,0:T(8,128)(2,1)} %copy-done.12) | copy-start | bytes 983044
  122.1 9.6 %copy-start.20 = (f32[320]{0:T(512)S(1)}, f32[320]{0:T(512)}, u32[]{:S(2)}) copy-start(f32[320]{0:T(512)} %copy-done.19) | copy-start | bytes 3844
  122.1 9.6 %copy-start.22 = (f32[320]{0:T(512)S(1)}, f32[320]{0:T(512)}, u32[]{:S(2)}) copy-start(f32[320]{0:T(512)} %copy-done.21) | copy-start | bytes 3844
  122.1 9.6 %copy-start.24 = (f32[320]{0:T(512)S(1)}, f32[320]{0:T(512)}, u32[]{:S(2)}) copy-start(f32[320]{0:T(512)} %copy-done.23) | copy-start | bytes 3844
  122.1 9.6 %copy-start.27 = (f32[320]{0:T(512)S(1)}, f32[320]{0:T(512)}, u32[]{:S(2)}) copy-start(f32[320]{0:T(512)} %copy-done.26) | copy-start | bytes 3844
  126.2 7.1 %copy-start.25 = (f32[320]{0:T(512)S(1)}, f32[320]{0:T(512)}, u32[]{:S(2)}) copy-start(f32[320]{0:T(512)} %convert_reduce_fusion) | copy-start | bytes 3844
  126.2 130.6 %copy-start.11 = (f32[512,320]{0,1:T(8,128)S(1)}, f32[512,320]{0,1:T(8,128)}, u32[]{:S(2)}) copy-start(f32[512,320]{0,1:T(8,128)} %copy.26) | copy-start | bytes 1966084
  126.2 130.6 %copy-start.14 = (bf16[512,320]{0,1:T(8,128)(2,1)S(1)}, bf16[512,320]{0,1:T(8,128)(2,1)}, u32[]{:S(2)}) copy-start(bf16[512,320]{0,1:T(8,128)(2,1)} %copy.24) | copy-start | bytes 983044
  128.9 129.7 %copy-start.28 = (u32[256]{0:T(256)S(1)}, u32[256]{0:T(256)}, u32[]{:S(2)}) copy-start(u32[256]{0:T(256)} %constant.25) | copy-start | bytes 3076
  257.4 9.7 %collective-permute-start.4 = (bf16[1,4,8,16,320]{4,3,2,1,0:T(8,128)(2,1)S(1)}, bf16[1,4,8,16,320]{4,3,2,1,0:T(8,128)(2,1)S(1)}, u32[]{:S(2)}, u32[]{:S(2)}) collective-permute-start(bf16[1,4,8,16,320]{4,3,2,1,0:T(8,128)(2,1)S(1)} %bitcast.295), channel_id=1, source_target_pairs={{64,0},{128,64},{192,128},{65,1},{129,65},{193,129},{66,2},{130,66... | collective-permute-start | bytes 983048 | tf_op jit(solution)/shard_map/ppermute | solution.py:55
  (4 other events, 13.6 us)
Sparse Core Ops, SparseCore 0:
  110.7 213.4 all-reduce.3
where the time goes:
time: 337 us; the launch traced here: 334 us
  blocking collectives  123 us (36%)
  matrix products  71.6 us (21%)
  waiting for transfers between devices  63.6 us (19%)
  local copies, waits for them, and re-layouts  27.1 us (8%)
  starting transfers between devices  23.5 us (7%)
  between operations  15.5 us (5%)
  other arithmetic  9.78 us (3%)
    psum x1, blocking collectives, in_one(): subtotal = lax.psum(jnp.concatenate([a.ravel() for a in arrays]), axis)  123 us
    unnamed x2, waiting for transfers between devices  57.1 us
    dot_general x27, matrix products, local(): lax.dot_general(window, kernel_all[kernel_idx], (((1,), (1,)), ((), ())),...  38.7 us
    dot_general x27, matrix products, local(): lax.dot_general(unit_rows, window, (((0,), (0,)), ((), ())), preferred_el...  32.9 us
    concatenate x1, local copies, waits for them, and re-layouts, local(): jnp.concatenate(weight_pieces, axis=0)  14 us
    all_to_all x1, starting transfers between devices, from_everyone(): lax.all_to_all(jnp.broadcast_to(shard[None], (count, *shard.shape)), axis...  12 us
    ppermute x2, starting transfers between devices, padded(): lax.ppermute(lax.slice_in_dim(block, block.shape[dim] - width, None, axis...  6.95 us
  transfers between devices with their start and end apart: 7, of which 2 were waited for; matrix products, arithmetic and copies ran while one was open for 12% of the time, Pallas kernels for 0%

commit v1 on v0

--- a/solution.py
+++ b/solution.py
@@ -5,6 +5,12 @@
 
 G = 32
 eps = 1e-05
+
+
+def gather_and_add(shard, name):
+    blocks = lax.all_gather(shard, name, axis=0, tiled=False)
+    result = blocks.sum(axis=0)
+    return result
 
 
 def from_everyone(shard, axis):
@@ -45,7 +51,7 @@
     ends = [0]
     for a in arrays:
         ends.append(ends[-1] + a.size)
-    subtotal = lax.psum(jnp.concatenate([a.ravel() for a in arrays]), axis)
+    subtotal = gather_and_add(jnp.concatenate([a.ravel() for a in arrays]), axis)
     return tuple((subtotal[b:e].reshape(a.shape) for a, b, e in zip(arrays, ends, ends[1:])))
 
 

time: 337 us -> 366 us (1.086)
  waiting for transfers between devices: 63.6 us -> 220 us
  blocking collectives: 123 us -> 0 us
  matrix products: 71.6 us -> 65.6 us
    unnamed x2, waiting for transfers between devices: 57.1 us -> 213 us
    psum x1 -> x0, blocking collectives: 123 us -> none  [in_one(): subtotal = lax.psum(jnp.concatenate([a.ravel() for a in arrays]), axis)]
    dot_general x27, matrix products: 32.9 us -> 29 us  [local(): lax.dot_general(unit_rows, window, (((0,), (0,)), ((), ())), preferred_el...]
  transfers between devices with their start and end apart: 7 -> 7, of which waited for: 2 -> 3; matrix products, arithmetic and copies ran while one was open for 12% -> 4% of each run, Pallas kernels for 0% -> 0%
where the time goes in v1:
time: 366 us; the launch traced here: 363 us
  waiting for transfers between devices  220 us (60%)
  matrix products  65.6 us (18%)
  local copies, waits for them, and re-layouts  26.9 us (7%)
  starting transfers between devices  23.5 us (6%)
  between operations  15.9 us (4%)
  other arithmetic  10.6 us (3%)
    unnamed x2, waiting for transfers between devices  213 us
    dot_general x27, matrix products, local(): lax.dot_general(window, kernel_all[kernel_idx], (((1,), (1,)), ((), ())),...  36.5 us
    dot_general x27, matrix products, local(): lax.dot_general(unit_rows, window, (((0,), (0,)), ((), ())), preferred_el...  29 us
    concatenate x1, local copies, waits for them, and re-layouts, local(): jnp.concatenate(weight_pieces, axis=0)  14 us
    all_to_all x1, starting transfers between devices, from_everyone(): lax.all_to_all(jnp.broadcast_to(shard[None], (count, *shard.shape)), axis...  12 us
  transfers between devices with their start and end apart: 7, of which 3 were waited for; matrix products, arithmetic and copies ran while one was open for 4% of the time, Pallas kernels for 0%

profile of v1, /device:TPU:2, one launch (start us, length us, event | category | flops | bytes accessed | tf_op | source)
XLA Modules:
  0.0 362.8 jit_solution(13786232980169760455)
XLA Ops:
  9.5 12.0 %all-to-all-start = ((f32[64,1,64]{2,1,0:T(1,128)}), f32[64,1,64]{2,1,0:T(1,128)S(1)}, u32[]{:S(2)}, u32[]{:S(2)}) async-start(f32[64,1,64]{2,1,0:T(1,128)} %broadcast_in_dim.10), calls=%async_computation | async-start | bytes 65536 | tf_op jit(solution)/shard_map/all_to_all | solution.py:18
  23.8 4.5 %collective-permute-start = (bf16[4,1,16,320]{3,2,1,0:T(8,128)(2,1)S(1)}, bf16[4,1,16,320]{3,2,1,0:T(8,128)(2,1)S(1)}, u32[]{:S(2)}, u32[]{:S(2)}) collective-permute-start(bf16[4,1,16,320]{3,2,1,0:T(8,128)(2,1)S(1)} %get-tuple-element.56), channel_id=1, source_target_pairs={{0,8},{8,16},{16,24},{24,32},{32,40},{40,48},{48,56},{1,9},{9,17},... | collective-permute-start | bytes 122888 | tf_op jit(solution)/shard_map/ppermute | solution.py:42
  32.0 1.3 fusion.73
  35.8 1.4 convolution_bitcast_fusion
  38.3 1.9 collective-permute-start.3
  40.2 2.4 collective-permute-start.2
  46.2 1.9 fusion.68
  48.5 1.3 fusion.38
  50.5 1.3 fusion.26
  58.4 1.3 convolution_add_fusion.22
  60.9 1.3 convolution_add_fusion.21
  63.4 1.3 convolution_add_fusion.20
  65.9 1.3 convolution_add_fusion.19
  73.5 1.3 convolution_add_fusion.16
  76.0 1.3 convolution_add_fusion.15
  78.5 1.3 fusion.3
  79.8 1.3 convolution_add_fusion.13
  83.6 1.3 convolution_add_fusion.11
  86.1 1.3 convolution_add_fusion.10
  88.6 1.3 fusion.2
  90.0 1.3 convolution_add_fusion.8
  92.5 1.3 convolution_add_fusion.7
  97.4 1.3 convolution_add_fusion.5
  100.0 1.3 convolution_add_fusion.4
  102.5 1.3 convolution_add_fusion.3
  105.0 1.5 convolution_add_fusion.2
  107.7 1.3 convolution_add_fusion.1
  110.2 2.3 multiply_reduce_fusion.1
  113.2 1.4 maximum_dynamic-update-slice_fusion
  114.6 14.0 %concatenate.39 = f32[8640,320]{0,1:T(8,128)} concatenate(f32[320,320]{0,1:T(8,128)S(1)} %fusion.74, f32[320,320]{0,1:T(8,128)} %fusion.75, f32[320,320]{0,1:T(8,128)} %fusion.76, f32[320,320]{0,1:T(8,128)} %fusion.77, f32[320,320]{0,1:T(8,128)} %fusion.78, f32[320,320]{0,1:T(8,128)} %fusion.79, f32[320,320]{0,1:T(8,128)} %fusion.80, f32[320,320]{0,1:T(8,128)} %fusion.81, ...), dimensions={0} | concatenate | bytes 22118400 | tf_op jit(solution)/shard_map/concatenate | solution.py:120
  128.9 213.1 %all-reduce.6.cloned.1.call-done = (f32[61440]{0:T(1024)}, f32[8640,320]{0,1:T(8,128)}) async-done(((f32[61440]{0:T(1024)}, f32[8640,320]{0,1:T(8,128)}), (f32[61440]{0:T(1024)}, f32[8640,320]{0,1:T(8,128)})) %all-reduce.6.cloned.1.call-update) | async-done | bytes 11304976
  349.0 6.2 %collective-permute-done.4 = bf16[1,4,8,16,320]{4,3,2,1,0:T(8,128)(2,1)S(1)} collective-permute-done((bf16[1,4,8,16,320]{4,3,2,1,0:T(8,128)(2,1)S(1)}, bf16[1,4,8,16,320]{4,3,2,1,0:T(8,128)(2,1)S(1)}, u32[]{:S(2)}, u32[]{:S(2)}) %collective-permute-start.4) | collective-permute-done | bytes 327712 | tf_op jit(solution)/shard_map/ppermute | solution.py:61
  (94 shorter events, 58.0 us)
Async XLA Ops:
  7.2 38.6 %copy-start = (bf16[1,4,8,16,320]{4,3,2,1,0:T(8,128)(2,1)S(1)}, bf16[1,4,8,16,320]{4,3,2,1,0:T(8,128)(2,1)}, u32[]{:S(2)}) copy-start(bf16[1,4,8,16,320]{4,3,2,1,0:T(8,128)(2,1)} %param.6) | copy-start | bytes 983044
  9.5 24.4 %all-to-all-start = ((f32[64,1,64]{2,1,0:T(1,128)}), f32[64,1,64]{2,1,0:T(1,128)S(1)}, u32[]{:S(2)}, u32[]{:S(2)}) async-start(f32[64,1,64]{2,1,0:T(1,128)} %broadcast_in_dim.10), calls=%async_computation | async-start | bytes 65536 | tf_op jit(solution)/shard_map/all_to_all | solution.py:18
  21.6 320.4 %all-reduce.6.cloned.1.call-start = ((), (), s32[]{:S(2)}) async-start(), calls=%async_computation.1 | async-start | bytes 22773760
  22.5 14.7 %collective-permute-start.1 = (bf16[4,1,16,320]{3,2,1,0:T(8,128)(2,1)S(1)}, bf16[4,1,16,320]{3,2,1,0:T(8,128)(2,1)S(1)}, u32[]{:S(2)}, u32[]{:S(2)}) collective-permute-start(bf16[4,1,16,320]{3,2,1,0:T(8,128)(2,1)S(1)} %get-tuple-element.57), channel_id=1, source_target_pairs={{8,0},{16,8},{24,16},{32,24},{40,32},{48,40},{56,48},{9,1},{17,9},... | collective-permute-start | bytes 122888 | tf_op jit(solution)/shard_map/ppermute | solution.py:45
  23.8 13.4 %collective-permute-start = (bf16[4,1,16,320]{3,2,1,0:T(8,128)(2,1)S(1)}, bf16[4,1,16,320]{3,2,1,0:T(8,128)(2,1)S(1)}, u32[]{:S(2)}, u32[]{:S(2)}) collective-permute-start(bf16[4,1,16,320]{3,2,1,0:T(8,128)(2,1)S(1)} %get-tuple-element.56), channel_id=1, source_target_pairs={{0,8},{8,16},{16,24},{24,32},{32,40},{40,48},{48,56},{1,9},{9,17},... | collective-permute-start | bytes 122888 | tf_op jit(solution)/shard_map/ppermute | solution.py:42
  38.3 6.4 %collective-permute-start.3 = (bf16[4,10,1,320]{3,2,1,0:T(2,128)(2,1)S(1)}, bf16[4,10,1,320]{3,2,1,0:T(2,128)(2,1)S(1)}, u32[]{:S(2)}, u32[]{:S(2)}) collective-permute-start(bf16[4,10,1,320]{3,2,1,0:T(2,128)(2,1)S(1)} %get-tuple-element.52), channel_id=1, source_target_pairs={{1,0},{2,1},{3,2},{4,3},{5,4},{6,5},{7,6},{9,8},{10,9},{11,10},{12... | collective-permute-start | bytes 76808 | tf_op jit(solution)/shard_map/ppermute | solution.py:45
  40.2 5.5 %collective-permute-start.2 = (bf16[4,10,1,320]{3,2,1,0:T(2,128)(2,1)S(1)}, bf16[4,10,1,320]{3,2,1,0:T(2,128)(2,1)S(1)}, u32[]{:S(2)}, u32[]{:S(2)}) collective-permute-start(bf16[4,10,1,320]{3,2,1,0:T(2,128)(2,1)S(1)} %get-tuple-element.53), channel_id=1, source_target_pairs={{0,1},{1,2},{2,3},{3,4},{4,5},{5,6},{6,7},{8,9},{9,10},{10,11},{11... | collective-permute-start | bytes 76808 | tf_op jit(solution)/shard_map/ppermute | solution.py:42
  128.6 215.3 %copy-start.1 = (f32[512,320]{0,1:T(8,128)S(1)}, f32[512,320]{0,1:T(8,128)}, u32[]{:S(2)}) copy-start(f32[512,320]{0,1:T(8,128)} %get-tuple-element.65) | copy-start | bytes 1966084
  344.4 10.8 %collective-permute-start.4 = (bf16[1,4,8,16,320]{4,3,2,1,0:T(8,128)(2,1)S(1)}, bf16[1,4,8,16,320]{4,3,2,1,0:T(8,128)(2,1)S(1)}, u32[]{:S(2)}, u32[]{:S(2)}) collective-permute-start(bf16[1,4,8,16,320]{4,3,2,1,0:T(8,128)(2,1)S(1)} %bitcast.296), channel_id=1, source_target_pairs={{64,0},{128,64},{192,128},{65,1},{129,65},{193,129},{66,2},{130,66... | collective-permute-start | bytes 983048 | tf_op jit(solution)/shard_map/ppermute | solution.py:61
Sparse Core Ops, SparseCore 0:
  128.8 213.1 all-reduce.5
